TPU v7x, 512 devices: a whole 4x8x8 slice. The times are simulated.
512 devices in a mesh: expert: 8 (over x, core), dp: 64 (over z, y).
Axes of the slice: x: 4, y: 8, z: 8, core: 2. Of those that a mesh axis runs over, the one named last changes fastest.
Arguments:
- tokens: bfloat16 [4096, 4096], P(('expert', 'dp')), may hold values from -6 to 6
- expert_ids: int32 [4096, 2], P(('expert', 'dp')), may hold values from 0 to 7, as said below
- slots: int32 [4096, 2], P(('expert', 'dp')), may hold values from -1 to 1, as said below
- mix_weights: float32 [4096, 2], P(('expert', 'dp')), may hold values from 0.1 to 1
- w_gate: bfloat16 [8, 4096, 8192], P('expert', None, 'dp'), may hold values from -0.09375 to 0.09375
- w_up: bfloat16 [8, 4096, 8192], P('expert', None, 'dp'), may hold values from -0.09375 to 0.09375
- w_down: bfloat16 [8, 8192, 4096], P('expert', None, 'dp'), may hold values from -0.0625 to 0.0625
Outputs:
- mixed: bfloat16 [4096, 4096], P(('expert', 'dp'))
Inputs may be any that keep to these rules, and one draw needn't show every extreme that they name: `expert_ids`: each token names 2 different experts. Within each aligned block of 8 tokens (the tokens of one device), the assignments to one expert get distinct slots among 0 to 1 in some order, at most 2 of them are kept and the others get -1; an expert with 2 or more assignments in the block has all 2 slots used. No two assignments of one block share an expert and a slot. In every block some expert has all 2 slots used.
All inputs are finite; a program needn't handle non-finite values.
Results may differ from a plain program's by a relative error of at most 0.0085.
Values may be sent and summed in bfloat16 or wider, within the bound.
No kernel may reach another device: no remote copies, remote signals or barrier semaphores. Data moves between devices by JAX's collectives and lax.ppermute only.
A program may use at most 128 MiB of HBM per device.

v0:
```python
import jax
import jax.numpy as jnp
from jax import lax
from jax.sharding import PartitionSpec as P

CAP = 2


def shards(tokens, expert_ids, slots, mix_weights, w_gate, w_up, w_down):
    tok_rows, model_width = tokens.shape
    experts = lax.axis_size("expert")
    capacity = CAP
    slot_count = experts * capacity
    slot_ids = jnp.arange(slot_count, dtype=jnp.int32)
    slot_expert = slot_ids // capacity
    slot_index = slot_ids % capacity
    matches = (expert_ids[None, :, :] == slot_expert[:, None, None]) & (
        slots[None, :, :] == slot_index[:, None, None]
    )
    occupied = jnp.any(matches, axis=2)
    dispatch_table = occupied.astype(jnp.bfloat16)
    outgoing = jnp.dot(dispatch_table, tokens, preferred_element_type=jnp.float32).astype(
        jnp.bfloat16
    )
    arrived = lax.all_to_all(outgoing, "expert", split_axis=0, concat_axis=0, tiled=True)
    gate_w = w_gate[0]
    up_w = w_up[0]
    down_w = w_down[0]
    portion = lax.all_gather(arrived, "dp", axis=0, tiled=True)
    gate_part = jnp.dot(portion, gate_w, preferred_element_type=jnp.float32)
    up_part = jnp.dot(portion, up_w, preferred_element_type=jnp.float32)
    hidden = (jax.nn.silu(gate_part) * up_part).astype(jnp.bfloat16)
    summed = jnp.dot(
        lax.all_gather(hidden, "dp", axis=1, tiled=True), down_w, preferred_element_type=jnp.float32
    )
    result = summed.astype(jnp.bfloat16)
    groups = lax.axis_size("dp")
    blocks = result.reshape(groups, experts, capacity, result.shape[1])
    blocks = lax.all_to_all(blocks, "expert", split_axis=1, concat_axis=1, tiled=True)
    blocks = lax.all_to_all(blocks, "dp", split_axis=0, concat_axis=3, tiled=True)
    returned = blocks.reshape(slot_count, model_width)
    weight_table = jnp.sum(jnp.where(matches, mix_weights[None, :, :], 0.0), axis=2)
    mixed = jnp.dot(
        weight_table.T, returned.astype(jnp.float32), preferred_element_type=jnp.float32
    )
    return mixed.astype(jnp.bfloat16)


def solution(mesh):
    placed = (
        P(("expert", "dp"), None),
        P(("expert", "dp"), None),
        P(("expert", "dp"), None),
        P(("expert", "dp"), None),
        P("expert", None, "dp"),
        P("expert", None, "dp"),
        P("expert", None, "dp"),
    )
    return jax.shard_map(
        shards, mesh=mesh, in_specs=placed, out_specs=P(("expert", "dp"), None), check_vma=False
    )
```

profile of v0, /device:TPU:1, one launch (start us, length us, event | category | flops | bytes accessed | tf_op | source)
XLA Modules:
  0.0 327.1 jit_solution(15211576409830812576)
XLA Ops:
  6.5 0.9 fusion.5
  7.5 1.1 convolution_convert_fusion
  8.5 0.1 all_to_all.22
  8.6 14.5 %all_to_all.32 = bf16[8,2,4096]{2,1,0:T(2,128)(2,1)S(1)} all-to-all(bf16[8,2,4096]{2,1,0:T(2,128)(2,1)S(1)} %all_to_all.22), channel_id=1, replica_groups=mesh['expert'=8,'dp'=64] {'expert'}, dimensions={0} | all-to-all | bytes 262144 | tf_op jit(solution)/shard_map/all_to_all | solution.py:25
  23.1 0.7 all_to_all.24
  23.8 0.0 all-gather.3.cloned.1.call-update
  23.8 0.0 all-gather.5.cloned.1.call-start
  23.9 98.3 %all-gather.3.cloned.1.call-done = bf16[1024,4096]{1,0:T(8,128)(2,1)} async-done(((bf16[16,4096]{1,0:T(8,128)(2,1)}), bf16[1024,4096]{1,0:T(8,128)(2,1)}) %all-gather.3.cloned.1.call-update) | async-done | bytes 8388624 | tf_op jit(solution)/shard_map/all_gather | solution.py:29
  122.2 5.8 %fusion.3 = f32[1024,128]{1,0:T(8,128)S(1)} fusion(bf16[1024,4096]{1,0:T(8,128)(2,1)} %all-gather.3.cloned.1.call-done, bf16[1,4096,128]{2,1,0:T(8,128)(2,1)S(1)} %copy-done), kind=kOutput, calls=%fused_computation.7 | convolution fusion | flops 1073741824 | bytes 9961472 | tf_op jit(solution)/shard_map/dot_general | solution.py:30
  128.1 0.0 copy-done.6
  128.1 0.0 copy-start.1
  128.1 3.0 fusion
  131.1 0.0 all-gather.5.cloned.1.call-update
  131.2 0.0 copy-start.2
  131.2 0.0 copy-start.3
  131.2 0.0 copy-start.4
  131.2 141.9 %all-gather.5.cloned.1.call-done = bf16[1024,8192]{1,0:T(8,128)(2,1)} async-done(((bf16[1024,128]{1,0:T(8,128)(2,1)}), bf16[1024,8192]{1,0:T(8,128)(2,1)}) %all-gather.5.cloned.1.call-update) | async-done | bytes 16777232 | tf_op jit(solution)/shard_map/all_gather | solution.py:34
  273.1 10.9 %convolution_convert_fusion.2 = bf16[1024,64]{0,1:T(8,128)(2,1)S(1)} fusion(bf16[1024,8192]{1,0:T(8,128)(2,1)} %all-gather.5.cloned.1.call-done, bf16[1,8192,64]{1,2,0:T(8,128)(2,1)S(1)} %copy-done.1), kind=kOutput, calls=%fused_computation.4 | convolution fusion | flops 1073807360 | bytes 17956864 | tf_op jit(solution)/shard_map/dot_general | solution.py:33
  284.1 0.2 copy.29
  284.3 0.2 copy.34
  284.4 0.2 reshape.36
  284.7 13.9 %all_to_all.33 = bf16[8,2,4096]{2,1,0:T(2,128)(2,1)S(1)} all-to-all(bf16[8,2,4096]{2,1,0:T(2,128)(2,1)S(1)} %reshape.36), channel_id=1, replica_groups=mesh['expert'=8,'dp'=64] {'expert'}, dimensions={0} | all-to-all | bytes 262144 | tf_op jit(solution)/shard_map/all_to_all | solution.py:39
  298.6 0.2 reshape.37
  298.9 0.2 copy.31
  299.0 0.8 reshape.38
  299.9 7.4 %all-to-all-start.2 = ((bf16[64,2,512]{2,1,0:T(2,128)(2,1)}), bf16[64,2,512]{2,1,0:T(2,128)(2,1)S(1)}, u32[]{:S(2)}, u32[]{:S(2)}) async-start(bf16[64,2,512]{2,1,0:T(2,128)(2,1)} %reshape.38), calls=%async_computation.2 | async-start | bytes 262144 | tf_op jit(solution)/shard_map/all_to_all | solution.py:40
  307.3 0.1 select_reduce_fusion
  307.4 11.5 %all-to-all-done.2 = bf16[64,2,512]{2,1,0:T(2,128)(2,1)S(1)} async-done(((bf16[64,2,512]{2,1,0:T(2,128)(2,1)}), bf16[64,2,512]{2,1,0:T(2,128)(2,1)S(1)}, u32[]{:S(2)}, u32[]{:S(2)}) %all-to-all-start.2) | async-done | bytes 131104 | tf_op jit(solution)/shard_map/all_to_all | solution.py:40
  318.9 0.2 reshape.39
  319.1 0.1 copy.32
  319.2 0.3 reshape.35
  319.4 0.8 fusion.6
  (11 shorter events, 0.0 us)
Async XLA Ops:
  6.5 115.7 %copy-start = (bf16[1,4096,128]{2,1,0:T(8,128)(2,1)S(1)}, bf16[1,4096,128]{2,1,0:T(8,128)(2,1)}, u32[]{:S(2)}) copy-start(bf16[1,4096,128]{2,1,0:T(8,128)(2,1)} %param.11) | copy-start | bytes 3145732
  6.5 121.5 %copy-start.6 = (bf16[1,4096,128]{2,1,0:T(8,128)(2,1)S(1)}, bf16[1,4096,128]{2,1,0:T(8,128)(2,1)}, u32[]{:S(2)}) copy-start(bf16[1,4096,128]{2,1,0:T(8,128)(2,1)} %param.12) | copy-start | bytes 3145732
  6.5 115.7 %all-gather.3.cloned.1.call-start = ((), (), s32[]{:S(2)}) async-start(), calls=%async_computation.3 | async-start | bytes 8519680 | tf_op jit(solution)/shard_map/all_gather | solution.py:29
  23.8 249.3 %all-gather.5.cloned.1.call-start = ((), (), s32[]{:S(2)}) async-start(), calls=%async_computation.4 | async-start | bytes 17039360 | tf_op jit(solution)/shard_map/all_gather | solution.py:34
  122.2 5.9 %copy-start.5 = (bf16[1024,4096]{1,0:T(8,128)(2,1)S(1)}, bf16[1024,4096]{1,0:T(8,128)(2,1)}, u32[]{:S(2)}) copy-start(bf16[1024,4096]{1,0:T(8,128)(2,1)} %all-gather.3.cloned.1.call-done) | copy-start | bytes 25165828
  128.1 145.1 %copy-start.1 = (bf16[1,8192,64]{1,2,0:T(8,128)(2,1)S(1)}, bf16[1,8192,64]{1,2,0:T(8,128)(2,1)}, u32[]{:S(2)}) copy-start(bf16[1,8192,64]{1,2,0:T(8,128)(2,1)} %param.13) | copy-start | bytes 3145732
  131.2 176.1 %copy-start.2 = (s32[8,2]{0,1:T(2,128)S(1)}, s32[8,2]{0,1:T(2,128)}, u32[]{:S(2)}) copy-start(s32[8,2]{0,1:T(2,128)} %param.9) | copy-start | bytes 196
  131.2 176.1 %copy-start.3 = (s32[8,2]{0,1:T(2,128)S(1)}, s32[8,2]{0,1:T(2,128)}, u32[]{:S(2)}) copy-start(s32[8,2]{0,1:T(2,128)} %param.8) | copy-start | bytes 196
  131.2 176.1 %copy-start.4 = (f32[8,2]{0,1:T(2,128)S(1)}, f32[8,2]{0,1:T(2,128)}, u32[]{:S(2)}) copy-start(f32[8,2]{0,1:T(2,128)} %param.10) | copy-start | bytes 196
  299.9 19.0 %all-to-all-start.2 = ((bf16[64,2,512]{2,1,0:T(2,128)(2,1)}), bf16[64,2,512]{2,1,0:T(2,128)(2,1)S(1)}, u32[]{:S(2)}, u32[]{:S(2)}) async-start(bf16[64,2,512]{2,1,0:T(2,128)(2,1)} %reshape.38), calls=%async_computation.2 | async-start | bytes 262144 | tf_op jit(solution)/shard_map/all_to_all | solution.py:40
Sparse Core Ops, SparseCore 0:
  24.0 98.1 all-gather.2
  131.3 141.7 all-gather.4
where the time goes:
time: 327 us
  waiting for transfers between devices  252 us (77%)
  blocking collectives  28.4 us (9%)
  matrix products  21.7 us (7%)
  between operations  13.6 us (4%)
  starting transfers between devices  7.4 us (2%)
    all_gather x1, waiting for transfers between devices, shards(): lax.all_gather(hidden, 'dp', axis=1, tiled=True)  142 us
    all_gather x1, waiting for transfers between devices, shards(): portion = lax.all_gather(arrived, 'dp', axis=0, tiled=True)  98.3 us
    all_to_all x1, blocking collectives, shards(): lax.all_to_all(outgoing, 'expert', split_axis=0, concat_axis=0, tiled=True)  14.5 us
    all_to_all x1, blocking collectives, shards(): lax.all_to_all(blocks, 'expert', split_axis=1, concat_axis=1, tiled=True)  13.9 us
    all_to_all x1, waiting for transfers between devices, shards(): lax.all_to_all(blocks, 'dp', split_axis=0, concat_axis=3, tiled=True)  11.5 us
    dot_general x1, matrix products, shards(): jnp.dot(lax.all_gather(hidden, 'dp', axis=1, tiled=True), down_w, preferr...  10.9 us
    all_to_all x1, starting transfers between devices, shards(): lax.all_to_all(blocks, 'dp', split_axis=0, concat_axis=3, tiled=True)  7.36 us
  transfers between devices with their start and end apart: 3, of which 3 were waited for; matrix products, arithmetic and copies ran while one was open for 0% of the time, Pallas kernels for 0%

commit v1 on v0

--- a/solution.py
+++ b/solution.py
@@ -4,6 +4,11 @@
 from jax.sharding import PartitionSpec as P
 
 CAP = 2
+
+
+def all_by_exchange(x, mesh_axis, along):
+    sent = jnp.stack([x] * lax.axis_size(mesh_axis))
+    return jnp.concatenate(lax.all_to_all(sent, mesh_axis, 0, 0), axis=along)
 
 
 def shards(tokens, expert_ids, slots, mix_weights, w_gate, w_up, w_down):
@@ -30,9 +35,7 @@
     gate_part = jnp.dot(portion, gate_w, preferred_element_type=jnp.float32)
     up_part = jnp.dot(portion, up_w, preferred_element_type=jnp.float32)
     hidden = (jax.nn.silu(gate_part) * up_part).astype(jnp.bfloat16)
-    summed = jnp.dot(
-        lax.all_gather(hidden, "dp", axis=1, tiled=True), down_w, preferred_element_type=jnp.float32
-    )
+    summed = jnp.dot(all_by_exchange(hidden, "dp", 1), down_w, preferred_element_type=jnp.float32)
     result = summed.astype(jnp.bfloat16)
     groups = lax.axis_size("dp")
     blocks = result.reshape(groups, experts, capacity, result.shape[1])

time: 327 us -> 589 us (1.80)
  blocking collectives: 28.4 us -> 405 us
  waiting for transfers between devices: 252 us -> 110 us
  starting transfers between devices: 7.4 us -> 37.7 us
  matrix products: 21.7 us -> 13.1 us
  local copies, waits for them, and re-layouts: 3.24 us -> 9.32 us
    all_to_all x0 -> x1, blocking collectives: none -> 378 us  [all_by_exchange(): return jnp.concatenate(lax.all_to_all(sent, mesh_axis, 0, 0), axis=along)]
    all_gather x1 -> x0, waiting for transfers between devices: 142 us -> none  [shards(): lax.all_gather(hidden, 'dp', axis=1, tiled=True)]
    all_to_all x1, starting transfers between devices: 7.36 us -> 37.7 us  [shards(): lax.all_to_all(blocks, 'dp', split_axis=0, concat_axis=3, tiled=True)]
    dot_general x1, matrix products: 10.9 us -> 3.02 us  [shards(): jnp.dot(all_by_exchange(hidden, 'dp', 1), down_w, preferred_element_type=...]
    another operation x0 -> x1, local copies, waits for them, and re-layouts: none -> 5.96 us  [all_by_exchange(): sent = jnp.stack([x] * lax.axis_size(mesh_axis))]
  transfers between devices with their start and end apart: 3 -> 2, of which waited for: 3 -> 2; matrix products, arithmetic and copies ran while one was open for 0% -> 0% of each run, Pallas kernels for 0% -> 0%
where the time goes in v1:
time: 589 us
  blocking collectives  405 us (69%)
  waiting for transfers between devices  110 us (19%)
  starting transfers between devices  37.7 us (6%)
  between operations  13.5 us (2%)
  matrix products  13.1 us (2%)
  local copies, waits for them, and re-layouts  9.32 us (2%)
    all_to_all x1, blocking collectives, all_by_exchange(): return jnp.concatenate(lax.all_to_all(sent, mesh_axis, 0, 0), axis=along)  378 us
    all_gather x1, waiting for transfers between devices, shards(): portion = lax.all_gather(arrived, 'dp', axis=0, tiled=True)  98.3 us
    all_to_all x1, starting transfers between devices, shards(): lax.all_to_all(blocks, 'dp', split_axis=0, concat_axis=3, tiled=True)  37.7 us
    all_to_all x1, blocking collectives, shards(): lax.all_to_all(outgoing, 'expert', split_axis=0, concat_axis=0, tiled=True)  14.5 us
    all_to_all x1, blocking collectives, shards(): lax.all_to_all(blocks, 'expert', split_axis=1, concat_axis=1, tiled=True)  11.8 us
  transfers between devices with their start and end apart: 2, of which 2 were waited for; matrix products, arithmetic and copies ran while one was open for 0% of the time, Pallas kernels for 0%

profile of v1, /device:TPU:1, one launch (start us, length us, event | category | flops | bytes accessed | tf_op | source)
XLA Modules:
  0.0 589.1 jit_solution(18329901595103180858)
XLA Ops:
  6.5 0.0 copy-start
  6.5 0.0 all-gather.2.cloned.1.call-start
  6.5 0.9 fusion.5
  7.5 1.1 convolution_convert_fusion
  8.5 0.1 all_to_all.25
  8.6 14.5 %all_to_all.37 = bf16[8,2,4096]{2,1,0:T(2,128)(2,1)S(1)} all-to-all(bf16[8,2,4096]{2,1,0:T(2,128)(2,1)S(1)} %all_to_all.25), channel_id=1, replica_groups=mesh['expert'=8,'dp'=64] {'expert'}, dimensions={0} | all-to-all | bytes 262144 | tf_op jit(solution)/shard_map/all_to_all | solution.py:30
  23.1 0.7 all_to_all.27
  23.8 0.0 all-gather.2.cloned.1.call-update
  23.8 98.3 %all-gather.2.cloned.1.call-done = bf16[1024,4096]{1,0:T(8,128)(2,1)} async-done(((bf16[16,4096]{1,0:T(8,128)(2,1)}), bf16[1024,4096]{1,0:T(8,128)(2,1)}) %all-gather.2.cloned.1.call-update) | async-done | bytes 8388624 | tf_op jit(solution)/shard_map/all_gather | solution.py:34
  122.2 0.0 copy-done
  122.2 5.9 fusion.3
  128.0 0.0 copy-done.6
  128.1 0.0 copy-done.5
  128.1 2.3 fusion
  130.4 0.1 copy.32
  130.6 6.0 %stack.2 = bf16[64,1024,128]{1,2,0:T(8,128)(2,1)} broadcast(bf16[1024,128]{0,1:T(8,128)(2,1)S(1)} %copy.32), dimensions={1,2} | broadcast | bytes 17039360 | tf_op jit(solution)/shard_map/stack | solution.py:10
  136.5 378.3 %all_to_all.38 = bf16[64,1024,128]{1,2,0:T(8,128)(2,1)S(1)} all-to-all(bf16[64,1024,128]{1,2,0:T(8,128)(2,1)} %stack.2), channel_id=1, replica_groups=mesh['expert'=8,'dp'=64] {'dp'}, dimensions={0} | all-to-all | bytes 33554432 | tf_op jit(solution)/shard_map/all_to_all | solution.py:11
  514.8 3.0 convolution_convert_fusion.2
  517.9 0.2 copy.33
  518.0 0.2 copy.38
  518.2 0.2 reshape.46
  518.5 11.8 %all_to_all.39 = bf16[8,2,4096]{2,1,0:T(2,128)(2,1)S(1)} all-to-all(bf16[8,2,4096]{2,1,0:T(2,128)(2,1)S(1)} %reshape.46), channel_id=1, replica_groups=mesh['expert'=8,'dp'=64] {'expert'}, dimensions={0} | all-to-all | bytes 262144 | tf_op jit(solution)/shard_map/all_to_all | solution.py:42
  530.3 0.2 reshape.47
  530.5 0.2 copy.35
  530.7 0.8 reshape.48
  531.6 37.7 %all-to-all-start.3 = ((bf16[64,2,512]{2,1,0:T(2,128)(2,1)}), bf16[64,2,512]{2,1,0:T(2,128)(2,1)S(1)}, u32[]{:S(2)}, u32[]{:S(2)}) async-start(bf16[64,2,512]{2,1,0:T(2,128)(2,1)} %reshape.48), calls=%async_computation.3 | async-start | bytes 262144 | tf_op jit(solution)/shard_map/all_to_all | solution.py:43
  569.3 0.1 select_reduce_fusion
  569.4 11.5 %all-to-all-done.3 = bf16[64,2,512]{2,1,0:T(2,128)(2,1)S(1)} async-done(((bf16[64,2,512]{2,1,0:T(2,128)(2,1)}), bf16[64,2,512]{2,1,0:T(2,128)(2,1)S(1)}, u32[]{:S(2)}, u32[]{:S(2)}) %all-to-all-start.3) | async-done | bytes 131104 | tf_op jit(solution)/shard_map/all_to_all | solution.py:43
  580.9 0.2 reshape.49
  581.1 0.1 copy.36
  581.2 0.3 reshape.45
  581.4 0.8 fusion.6
  (11 shorter events, 0.0 us)
Async XLA Ops:
  6.5 115.6 %copy-start = (bf16[1,4096,128]{2,1,0:T(8,128)(2,1)S(1)}, bf16[1,4096,128]{2,1,0:T(8,128)(2,1)}, u32[]{:S(2)}) copy-start(bf16[1,4096,128]{2,1,0:T(8,128)(2,1)} %param.11) | copy-start | bytes 3145732
  6.5 121.5 %copy-start.6 = (bf16[1,4096,128]{2,1,0:T(8,128)(2,1)S(1)}, bf16[1,4096,128]{2,1,0:T(8,128)(2,1)}, u32[]{:S(2)}) copy-start(bf16[1,4096,128]{2,1,0:T(8,128)(2,1)} %param.12) | copy-start | bytes 3145732
  6.5 115.6 %all-gather.2.cloned.1.call-start = ((), (), s32[]{:S(2)}) async-start(), calls=%async_computation.4 | async-start | bytes 8519680 | tf_op jit(solution)/shard_map/all_gather | solution.py:34
  122.2 5.9 copy-start.5
  136.5 378.3 %copy-start.1 = (bf16[1,8192,64]{1,2,0:T(8,128)(2,1)S(1)}, bf16[1,8192,64]{1,2,0:T(8,128)(2,1)}, u32[]{:S(2)}) copy-start(bf16[1,8192,64]{1,2,0:T(8,128)(2,1)} %param.13) | copy-start | bytes 3145732
  514.8 54.4 %copy-start.2 = (s32[8,2]{0,1:T(2,128)S(1)}, s32[8,2]{0,1:T(2,128)}, u32[]{:S(2)}) copy-start(s32[8,2]{0,1:T(2,128)} %param.9) | copy-start | bytes 196
  514.8 54.4 %copy-start.3 = (s32[8,2]{0,1:T(2,128)S(1)}, s32[8,2]{0,1:T(2,128)}, u32[]{:S(2)}) copy-start(s32[8,2]{0,1:T(2,128)} %param.8) | copy-start | bytes 196
  514.8 54.4 %copy-start.4 = (f32[8,2]{0,1:T(2,128)S(1)}, f32[8,2]{0,1:T(2,128)}, u32[]{:S(2)}) copy-start(f32[8,2]{0,1:T(2,128)} %param.10) | copy-start | bytes 196
  531.6 49.3 %all-to-all-start.3 = ((bf16[64,2,512]{2,1,0:T(2,128)(2,1)}), bf16[64,2,512]{2,1,0:T(2,128)(2,1)S(1)}, u32[]{:S(2)}, u32[]{:S(2)}) async-start(bf16[64,2,512]{2,1,0:T(2,128)(2,1)} %reshape.48), calls=%async_computation.3 | async-start | bytes 262144 | tf_op jit(solution)/shard_map/all_to_all | solution.py:43
Sparse Core Ops, SparseCore 0:
  23.9 98.1 all-gather.1
